TPU v7x, 32 devices: a whole 2x2x4 slice. The times are simulated.
32 devices in a mesh: dp: 4 (over x, core), mp: 8 (over z, y).
Axes of the slice: x: 2, y: 2, z: 4, core: 2. Of those that a mesh axis runs over, the one named last changes fastest.
Arguments:
- tokens: bfloat16 [3072, 6144], P('dp'), may hold values from -60 to 60
- ln_gain: float32 [6144], replicated, may hold values from 0.1 to 1.9
- w_qkv: bfloat16 [6144, 3, 6144], P('dp', None, 'mp'), may hold values from -1 to 1
- q_gain: float32 [128], replicated, may hold values from 0.7 to 2
- k_gain: float32 [128], replicated, may hold values from 0.7 to 2
Outputs:
- context: bfloat16 [3072, 6144], P('dp', 'mp')
All inputs are finite; a program needn't handle non-finite values.
Results may differ from a plain program's by a relative error of at most 0.012.
The roundings to bfloat16 on the way count: a program that leaves them out, or rounds other values in their place, can miss the bound.
Values may be sent and summed in bfloat16 or wider, within the bound.
A program may use at most 128 MiB of HBM per device.

v0:
```python
import functools

import jax
import jax.numpy as jnp
from jax import lax
from jax.experimental import pallas as pl
from jax.experimental.pallas import tpu as pltpu
from jax.sharding import PartitionSpec as P


HEADS = 48
HEAD_DIM = 128
PATCHES = 256
SPLITS = 4


norm_eps = 1e-06


def from_behind(shard, axis, by):
    length = lax.axis_size(axis)
    return lax.ppermute(shard, axis, [(i, (i + by) % length) for i in range(length)])


def layer_norm(values, gain_vector):
    centre = jnp.mean(values, axis=-1, keepdims=True)
    centred = values - centre
    spread = jnp.mean(centred * centred, axis=-1, keepdims=True)
    return centred * lax.rsqrt(spread + norm_eps) * gain_vector


def head_norm(pieces, gain_rows):
    values = pieces.astype(jnp.float32)
    centre = jnp.mean(values, axis=(0, 4), keepdims=True)
    centred = values - centre
    spread = jnp.mean(centred * centred, axis=(0, 4), keepdims=True)
    return centred * lax.rsqrt(spread + norm_eps) * gain_rows[:, None, None, None, :]


def ordered_gains(gain_vector, quarter_order):
    gain_table = gain_vector.reshape(SPLITS, -1)
    selector = (quarter_order[:, None] == jnp.arange(SPLITS, dtype=jnp.int32)[None, :]).astype(
        jnp.float32
    )
    return jnp.dot(selector, gain_table, precision=lax.Precision.HIGHEST)


def plain_body(tokens, ln_gain, w_qkv, q_gain, k_gain):
    local_rows = tokens.shape[0]
    normed = layer_norm(tokens.astype(jnp.float32), ln_gain).astype(jnp.bfloat16)
    flat_weight = w_qkv.reshape(w_qkv.shape[0], -1)
    out_width = flat_weight.shape[1]
    row_piece = lax.all_gather(w_qkv, "dp", axis=0, tiled=True)
    partial_value = jnp.dot(
        normed, row_piece.reshape(row_piece.shape[0], out_width), preferred_element_type=jnp.float32
    )
    projected = partial_value.astype(jnp.bfloat16)
    groups = lax.axis_size("mp") // SPLITS
    head_count = HEADS // groups
    quarter_rows = PATCHES // SPLITS
    my_quarter = lax.axis_index("mp") // groups
    images = local_rows // PATCHES
    head_view = projected.reshape(images, PATCHES, 3, head_count, HEAD_DIM // SPLITS)
    queries = head_view[:, :, 0]
    keys_vals = head_view[:, :, 1:]
    counting = jnp.arange(SPLITS, dtype=jnp.int32)
    own_rows = lax.dynamic_slice_in_dim(queries, my_quarter * quarter_rows, quarter_rows, 1)
    query_list = [own_rows]
    pair_list = [keys_vals]
    for offset in range(1, SPLITS):
        outgoing = lax.dynamic_slice_in_dim(
            queries, (my_quarter + offset) % SPLITS * quarter_rows, quarter_rows, 1
        )
        got_query, got_pair = from_behind((outgoing, keys_vals), "mp", offset * groups)
        query_list.append(got_query)
        pair_list.append(got_pair)
    query_pieces = jnp.stack(query_list, 0)
    pair_pieces = jnp.stack(pair_list, 0)
    quarter_order = (my_quarter - counting) % SPLITS
    query_normed = (
        head_norm(query_pieces, ordered_gains(q_gain, quarter_order)) * HEAD_DIM ** (-0.5)
    ).astype(jnp.bfloat16)
    key_normed = head_norm(pair_pieces[:, :, :, 0], ordered_gains(k_gain, quarter_order)).astype(
        jnp.bfloat16
    )
    value_part = pair_pieces[:, :, :, 1]
    scores = jnp.einsum(
        "sirhe,sikhe->ihrk", query_normed, key_normed, preferred_element_type=jnp.float32
    )
    raised = jnp.exp(scores)
    weights = (raised / jnp.sum(raised, axis=-1, keepdims=True)).astype(jnp.bfloat16)
    context = jnp.einsum(
        "ihrk,sikhe->sirhe", weights, value_part, preferred_element_type=jnp.float32
    ).astype(jnp.bfloat16)
    rows_list = [context[0]]
    for offset in range(1, SPLITS):
        wanted = (my_quarter - offset) % SPLITS
        slot_index = jnp.sum(jnp.where(quarter_order == wanted, counting, 0))
        outgoing = lax.dynamic_index_in_dim(context, slot_index, 0, keepdims=False)
        rows_list.append(from_behind(outgoing, "mp", (SPLITS - offset) * groups))
    own_block = jnp.roll(jnp.concatenate(rows_list, 1), my_quarter * quarter_rows, axis=1)
    return own_block.reshape(local_rows, -1)

MESH = pl.DeviceIdType.MESH
VMEM_LIMIT = 62 * 1024 * 1024
KINDS = 3
BLOCK = 256
SHARERS = 4
LAG_SUM, LAG_ATTEND, LAG_STORE = 1, 3, 5


def column_norm(values, gain_column):
    centre = jnp.mean(values, axis=0, keepdims=True)
    centred = values - centre
    spread = jnp.mean(centred * centred, axis=0, keepdims=True)
    return centred * lax.rsqrt(spread + norm_eps) * gain_column


def span(start, size):
    return pl.ds(pl.multiple_of(start, size), size)


def fused_kernel(
    token_hbm, gain_ref, weight_hbm, q_gain_ref, k_gain_ref, out_ref,
    work, weight, own, other, share, total, partial, pieces, returned,
    token_in, weight_in, weight_out, weight_got, share_out, share_got,
    relay_out, relay_got, partial_out, partial_got, piece_out, piece_got,
    context_out, context_got,
):
    dp, mp = lax.axis_index("dp"), lax.axis_index("mp")
    groups = lax.axis_size("mp") // SPLITS
    side, core = dp // 2, dp % 2
    quarter, group = mp // groups, mp % groups
    rows, features = token_hbm.shape
    width = weight_hbm.shape[2]
    depth = weight_hbm.shape[1]
    half = features // 2
    images, blocks = rows // PATCHES, width // BLOCK
    chunks = images * blocks
    part = HEAD_DIM // SPLITS
    height = BLOCK // SPLITS
    heads = height // part
    share_rows = PATCHES // SHARERS

    sibling = (side * 2 + 1 - core, mp)
    across = ((1 - side) * 2 + core, mp)
    near_group = (dp, quarter * groups + 1 - group)
    pair = quarter + 1 - 2 * (quarter % 2)
    near_quarter = (dp, pair * groups + group)
    diagonal = (dp, pair * groups + 1 - group)
    relays = (near_group, near_quarter, diagonal)

    def quarter_at(offset):
        return (dp, (quarter + offset) % SPLITS * groups + group)

    def remote(source, target, send, receive, device):
        return pltpu.make_async_remote_copy(
            src_ref=source, dst_ref=target, send_sem=send, recv_sem=receive,
            device_id=device, device_id_type=MESH,
        )

    def token_load(image):
        lines = span(image * PATCHES, PATCHES)
        return pltpu.make_async_copy(token_hbm.at[lines], work.at[lines], token_in.at[image])

    mine = span(core * depth, depth)

    def weight_load(block):
        columns = span(block * BLOCK, BLOCK)
        return pltpu.make_async_copy(
            weight_hbm.at[:, :, columns], weight.at[:, mine, columns], weight_in.at[block]
        )

    def weight_send(block):
        columns = span(block * BLOCK, BLOCK)
        return remote(
            weight_hbm.at[:, :, columns], weight.at[:, mine, columns],
            weight_out.at[block], weight_got.at[block], sibling,
        )

    place = quarter % 2 * 2 + group

    def share_send(image):
        return remote(
            share.at[image], other.at[span(image * PATCHES + place * share_rows, share_rows)],
            share_out.at[image], share_got.at[image], across,
        )

    def relay_send(image, way):
        lines = span(image * PATCHES + place * share_rows, share_rows)
        return remote(
            other.at[lines], other.at[lines],
            relay_out.at[image * 3 + way], relay_got.at[image * 3 + way], relays[way],
        )

    def partial_send(chunk):
        image, block = chunk // blocks, chunk % blocks
        return remote(
            work.at[span(image * PATCHES, PATCHES), span(block * KINDS * BLOCK, KINDS * BLOCK)],
            partial.at[chunk], partial_out.at[chunk], partial_got.at[chunk], across,
        )

    def piece_source(chunk, destination):
        image, block = chunk // blocks, chunk % blocks
        first = KINDS * width
        return work.at[
            span(image * PATCHES + destination * height, height),
            span(first + block * KINDS * BLOCK, KINDS * BLOCK),
        ]

    def piece_send(chunk, offset):
        slot = chunk * 3 + offset - 1
        return remote(
            piece_source(chunk, (quarter + offset) % SPLITS), pieces.at[chunk, quarter],
            piece_out.at[slot], piece_got.at[slot], quarter_at(offset),
        )

    def context_source(chunk, destination):
        image, block = chunk // blocks, chunk % blocks
        first = 2 * KINDS * width
        return work.at[
            span(image * PATCHES + destination * height, height),
            span(first + block * BLOCK, BLOCK),
        ]

    def context_send(chunk, offset):
        slot = chunk * 3 + offset - 1
        return remote(
            context_source(chunk, (quarter + offset) % SPLITS), returned.at[chunk, quarter],
            context_out.at[slot], context_got.at[slot], quarter_at(offset),
        )

    for image in range(images):
        token_load(image).start()
    for block in range(blocks):
        weight_load(block).start()
    barrier = pltpu.get_barrier_semaphore()
    partners = [sibling, across, near_group, diagonal] + [quarter_at(o) for o in range(1, SPLITS)]
    for partner in partners:
        pl.semaphore_signal(barrier, inc=1, device_id=partner, device_id_type=MESH)
    pl.semaphore_wait(barrier, len(partners))
    for block in range(blocks):
        weight_send(block).start()

    own_half = span(side * half, half)
    other_half = span((1 - side) * half, half)

    def normalize(image, turn, sharing):
        lines = span(image * PATCHES + (place + turn) % SHARERS * share_rows, share_rows)
        values = work[lines, :].astype(jnp.float32)
        centre = jnp.mean(values, axis=-1, keepdims=True)
        centred = values - centre
        spread = jnp.mean(centred * centred, axis=-1, keepdims=True)
        scale = lax.rsqrt(spread + norm_eps)

        def scaled(columns):
            return (
                (work[lines, columns].astype(jnp.float32) - centre) * scale * gain_ref[:, columns]
            ).astype(jnp.bfloat16)

        if sharing:
            share[image] = scaled(other_half)
        own[lines, :] = scaled(own_half)

    def first_norm(image, carry):
        token_load(image).wait()
        normalize(image, 0, True)
        share_send(image).start()
        return carry

    lax.fori_loop(0, images, first_norm, 0)

    def later_norm(step, carry):
        normalize(step // (SHARERS - 1), step % (SHARERS - 1) + 1, False)
        return carry

    lax.fori_loop(0, images * (SHARERS - 1), later_norm, 0)

    def relay(image):
        share_send(image).wait_recv()
        for way in range(3):
            relay_send(image, way).start()

    def own_part(step, carry):
        block, kind = step // KINDS, step % KINDS

        @pl.when(kind == 0)
        def _():
            weight_load(block).wait()
            weight_send(block).wait_recv()

        total[:, span(step * BLOCK, BLOCK)] = jnp.dot(
            own[...], weight[kind, :, span(block * BLOCK, BLOCK)],
            preferred_element_type=jnp.float32,
        )

        @pl.when(kind == KINDS - 1)
        def _():
            relay(block)

        return carry

    lax.fori_loop(0, blocks * KINDS, own_part, 0)

    def send_partial(chunk):
        image, block = chunk // blocks, chunk % blocks

        @pl.when(block == 0)
        def _():
            for way in range(3):
                relay_send(image, way).wait_recv()

        lines = span(image * PATCHES, PATCHES)
        for kind in range(KINDS):
            term = jnp.dot(
                other[lines, :], weight[kind, :, span(block * BLOCK, BLOCK)],
                preferred_element_type=jnp.float32,
            )
            work[lines, span((block * KINDS + kind) * BLOCK, BLOCK)] = term.astype(jnp.bfloat16)
        partial_send(chunk).start()

    def sum_up(chunk):
        image, block = chunk // blocks, chunk % blocks
        partial_send(chunk).wait_recv()
        lines = span(image * PATCHES, PATCHES)
        first = KINDS * width
        for kind in range(KINDS):
            columns = (block * KINDS + kind) * BLOCK
            whole = total[lines, span(columns, BLOCK)] + partial[
                chunk, :, kind * BLOCK : (kind + 1) * BLOCK
            ].astype(jnp.float32)
            work[lines, span(first + columns, BLOCK)] = whole.T.astype(jnp.bfloat16)
        for offset in range(1, SPLITS):
            piece_send(chunk, offset).start()
        pieces[chunk, quarter] = piece_source(chunk, quarter)[...]

    def attend(chunk):
        image, block = chunk // blocks, chunk % blocks
        for offset in range(1, SPLITS):
            source = (quarter - offset + SPLITS) % SPLITS
            slot = chunk * 3 + offset - 1
            remote(
                pieces.at[chunk, source], pieces.at[chunk, source],
                piece_out.at[slot], piece_got.at[slot], quarter_at(offset),
            ).wait_recv()
        for head in range(heads):
            def gathered(kind):
                return jnp.concatenate(
                    [
                        pieces[
                            chunk, source, head * part : (head + 1) * part,
                            kind * BLOCK : (kind + 1) * BLOCK,
                        ]
                        for source in range(SPLITS)
                    ],
                    axis=0,
                )

            query = (
                column_norm(gathered(0).astype(jnp.float32), q_gain_ref[...]) * HEAD_DIM ** (-0.5)
            ).astype(jnp.bfloat16)
            key = column_norm(gathered(1).astype(jnp.float32), k_gain_ref[...]).astype(jnp.bfloat16)
            scores = lax.dot_general(
                key, query, (((0,), (0,)), ((), ())), preferred_element_type=jnp.float32
            )
            raised = jnp.exp(scores)
            weights = (raised / jnp.sum(raised, axis=0, keepdims=True)).astype(jnp.bfloat16)
            attended = jnp.dot(gathered(2), weights, preferred_element_type=jnp.float32).astype(
                jnp.bfloat16
            )
            columns = span(2 * KINDS * width + block * BLOCK, BLOCK)
            for target in range(SPLITS):
                line = image * PATCHES + target * height + head * part
                work[span(line, part), columns] = attended[target * part : (target + 1) * part]
        for offset in range(1, SPLITS):
            context_send(chunk, offset).start()
        returned[chunk, quarter] = context_source(chunk, quarter)[...]

    def store(chunk):
        image, block = chunk // blocks, chunk % blocks
        for offset in range(1, SPLITS):
            source = (quarter - offset + SPLITS) % SPLITS
            slot = chunk * 3 + offset - 1
            remote(
                returned.at[chunk, source], returned.at[chunk, source],
                context_out.at[slot], context_got.at[slot], quarter_at(offset),
            ).wait_recv()
        upright = returned[chunk].reshape(BLOCK, PATCHES)
        out_ref[span(image * PATCHES, PATCHES), span(block * BLOCK, BLOCK)] = upright.T

    def step(turn, carry):
        for lag, stage in (
            (0, send_partial), (LAG_SUM, sum_up), (LAG_ATTEND, attend), (LAG_STORE, store)
        ):
            @pl.when((turn >= lag) & (turn < chunks + lag))
            def _(lag=lag, stage=stage):
                stage(turn - lag)

        return carry

    lax.fori_loop(0, chunks + LAG_STORE, step, 0)

    for block in range(blocks):
        weight_send(block).wait_send()

    def drain(image, carry):
        share_send(image).wait_send()
        for way in range(3):
            relay_send(image, way).wait_send()
        return carry

    lax.fori_loop(0, images, drain, 0)

    def drain_chunk(chunk, carry):
        partial_send(chunk).wait_send()
        for offset in range(1, SPLITS):
            piece_send(chunk, offset).wait_send()
            context_send(chunk, offset).wait_send()
        return carry

    lax.fori_loop(0, chunks, drain_chunk, 0)


def fused(tokens, gain, weights, q_gain, k_gain):
    rows, features = tokens.shape
    kinds, depth, width = weights.shape
    images, blocks = rows // PATCHES, width // BLOCK
    chunks = images * blocks
    height = BLOCK // SPLITS
    whole = pl.BlockSpec(memory_space=pltpu.VMEM)
    outside = pl.BlockSpec(memory_space=pl.ANY)
    dma = pltpu.SemaphoreType.DMA

    def vmem(*shape, dtype=jnp.bfloat16):
        return pltpu.VMEM(shape, dtype)

    return pl.pallas_call(
        fused_kernel,
        out_shape=jax.ShapeDtypeStruct((rows, width), jnp.bfloat16),
        in_specs=[outside, whole, outside, whole, whole],
        out_specs=whole,
        scratch_shapes=[
            vmem(rows, features),
            vmem(kinds, 2 * depth, width),
            vmem(rows, features // 2),
            vmem(rows, features // 2),
            vmem(images, PATCHES // SHARERS, features // 2),
            vmem(rows, kinds * width, dtype=jnp.float32),
            vmem(chunks, PATCHES, kinds * BLOCK),
            vmem(chunks, SPLITS, height, kinds * PATCHES),
            vmem(chunks, SPLITS, height, PATCHES),
            dma((images,)), dma((blocks,)),
            dma((blocks,)), dma((blocks,)),
            dma((images,)), dma((images,)),
            dma((images * 3,)), dma((images * 3,)),
            dma((chunks,)), dma((chunks,)),
            dma((chunks * 3,)), dma((chunks * 3,)),
            dma((chunks * 3,)), dma((chunks * 3,)),
        ],
        compiler_params=pltpu.CompilerParams(
            collective_id=0, has_side_effects=True, vmem_limit_bytes=VMEM_LIMIT
        ),
        name="fused",
    )(tokens, gain.reshape(1, features), weights, q_gain.reshape(HEAD_DIM, 1),
      k_gain.reshape(HEAD_DIM, 1))


def body(tokens, ln_gain, w_qkv, q_gain, k_gain):
    return fused(tokens, ln_gain, jnp.transpose(w_qkv, (1, 0, 2)), q_gain, k_gain)


def solution(mesh):
    local_heads = HEADS * SPLITS // mesh.shape["mp"]
    columns = local_heads * (HEAD_DIM // SPLITS)
    fits = columns % BLOCK == 0 and mesh.shape["mp"] == 2 * SPLITS
    fits = fits and mesh.shape["dp"] == 4
    return jax.shard_map(
        body if fits else plain_body,
        mesh=mesh,
        in_specs=(P("dp", None), P(), P("dp", None, "mp"), P(), P()),
        out_specs=P("dp", "mp"),
        check_vma=False,
    )
```

profile of v0, /device:TPU:0, one launch (start us, length us, event | category | flops | bytes accessed | tf_op | source)
XLA Modules:
  0.0 169.9 jit_solution(10566899260852677214)
XLA Ops:
  0.0 1.4 copy.6.q_gain_ref
  1.4 1.4 copy.7.k_gain_ref
  2.8 164.8 %fused.1 = bf16[768,768]{1,0:T(8,128)(2,1)} custom-call(bf16[768,6144]{1,0:T(8,128)(2,1)} %token_hbm.1, f32[1,6144]{1,0:T(1,128)} %bitcast.5, bf16[3,1536,768]{2,1,0:T(8,128)(2,1)} %bitcast.4, f32[128,1]{1,0:T(8,128)} %copy.6.q_gain_ref, f32[128,1]{1,0:T(8,128)} %copy.7.k_gain_ref), custom_call_target="tpu_custom_call" | custom-call | tf_op jit(solution)/shard_map/fused/pallas_call | solution.py:437
  167.6 2.4 %copy.9 = bf16[768,768]{1,0:T(8,128)(2,1)} copy(bf16[768,768]{1,0:T(8,128)(2,1)} %fused.1) | data formatting | bytes 2359296
where the time goes:
time: 170 us
  Pallas kernels  165 us (97%)
  local copies, waits for them, and re-layouts  5.13 us (3%)
    pallas_call x1, Pallas kernels, fused(): pl.pallas_call(fused_kernel, out_shape=jax.ShapeDtypeStruct((rows, width)...  165 us

commit v1 on v0

v1 whole, which is shorter than its diff:
```python
import functools

import jax
import jax.numpy as jnp
from jax import lax
from jax.experimental import pallas as pl
from jax.experimental.pallas import tpu as pltpu
from jax.sharding import PartitionSpec as P


HEADS = 48
HEAD_DIM = 128
PATCHES = 256
SPLITS = 4


norm_eps = 1e-06


def from_behind(shard, axis, by):
    length = lax.axis_size(axis)
    return lax.ppermute(shard, axis, [(i, (i + by) % length) for i in range(length)])


def layer_norm(values, gain_vector):
    centre = jnp.mean(values, axis=-1, keepdims=True)
    centred = values - centre
    spread = jnp.mean(centred * centred, axis=-1, keepdims=True)
    return centred * lax.rsqrt(spread + norm_eps) * gain_vector


def head_norm(pieces, gain_rows):
    values = pieces.astype(jnp.float32)
    centre = jnp.mean(values, axis=(0, 4), keepdims=True)
    centred = values - centre
    spread = jnp.mean(centred * centred, axis=(0, 4), keepdims=True)
    return centred * lax.rsqrt(spread + norm_eps) * gain_rows[:, None, None, None, :]


def ordered_gains(gain_vector, quarter_order):
    gain_table = gain_vector.reshape(SPLITS, -1)
    selector = (quarter_order[:, None] == jnp.arange(SPLITS, dtype=jnp.int32)[None, :]).astype(
        jnp.float32
    )
    return jnp.dot(selector, gain_table, precision=lax.Precision.HIGHEST)


def plain_body(tokens, ln_gain, w_qkv, q_gain, k_gain):
    local_rows = tokens.shape[0]
    normed = layer_norm(tokens.astype(jnp.float32), ln_gain).astype(jnp.bfloat16)
    flat_weight = w_qkv.reshape(w_qkv.shape[0], -1)
    out_width = flat_weight.shape[1]
    row_piece = lax.all_gather(w_qkv, "dp", axis=0, tiled=True)
    partial_value = jnp.dot(
        normed, row_piece.reshape(row_piece.shape[0], out_width), preferred_element_type=jnp.float32
    )
    projected = partial_value.astype(jnp.bfloat16)
    groups = lax.axis_size("mp") // SPLITS
    head_count = HEADS // groups
    quarter_rows = PATCHES // SPLITS
    my_quarter = lax.axis_index("mp") // groups
    images = local_rows // PATCHES
    head_view = projected.reshape(images, PATCHES, 3, head_count, HEAD_DIM // SPLITS)
    queries = head_view[:, :, 0]
    keys_vals = head_view[:, :, 1:]
    counting = jnp.arange(SPLITS, dtype=jnp.int32)
    own_rows = lax.dynamic_slice_in_dim(queries, my_quarter * quarter_rows, quarter_rows, 1)
    query_list = [own_rows]
    pair_list = [keys_vals]
    for offset in range(1, SPLITS):
        outgoing = lax.dynamic_slice_in_dim(
            queries, (my_quarter + offset) % SPLITS * quarter_rows, quarter_rows, 1
        )
        got_query, got_pair = from_behind((outgoing, keys_vals), "mp", offset * groups)
        query_list.append(got_query)
        pair_list.append(got_pair)
    query_pieces = jnp.stack(query_list, 0)
    pair_pieces = jnp.stack(pair_list, 0)
    quarter_order = (my_quarter - counting) % SPLITS
    query_normed = (
        head_norm(query_pieces, ordered_gains(q_gain, quarter_order)) * HEAD_DIM ** (-0.5)
    ).astype(jnp.bfloat16)
    key_normed = head_norm(pair_pieces[:, :, :, 0], ordered_gains(k_gain, quarter_order)).astype(
        jnp.bfloat16
    )
    value_part = pair_pieces[:, :, :, 1]
    scores = jnp.einsum(
        "sirhe,sikhe->ihrk", query_normed, key_normed, preferred_element_type=jnp.float32
    )
    raised = jnp.exp(scores)
    weights = (raised / jnp.sum(raised, axis=-1, keepdims=True)).astype(jnp.bfloat16)
    context = jnp.einsum(
        "ihrk,sikhe->sirhe", weights, value_part, preferred_element_type=jnp.float32
    ).astype(jnp.bfloat16)
    rows_list = [context[0]]
    for offset in range(1, SPLITS):
        wanted = (my_quarter - offset) % SPLITS
        slot_index = jnp.sum(jnp.where(quarter_order == wanted, counting, 0))
        outgoing = lax.dynamic_index_in_dim(context, slot_index, 0, keepdims=False)
        rows_list.append(from_behind(outgoing, "mp", (SPLITS - offset) * groups))
    own_block = jnp.roll(jnp.concatenate(rows_list, 1), my_quarter * quarter_rows, axis=1)
    return own_block.reshape(local_rows, -1)

MESH = pl.DeviceIdType.MESH
VMEM_LIMIT = 62 * 1024 * 1024
BLOCK = 256
PIECES = 4
GROUPS = 2
UNITS = 9
CHUNKS = "abd"


def column_norm(values, gain):
    centre = jnp.mean(values, axis=0, keepdims=True)
    centred = values - centre
    spread = jnp.mean(centred * centred, axis=0, keepdims=True)
    return centred * lax.rsqrt(spread + norm_eps) * gain


def span(start, size):
    return pl.ds(pl.multiple_of(start, size), size)


def fused_kernel(
    token_hbm, gain_ref, weight_hbm, q_gain_ref, k_gain_ref, out_ref,
    work, weight, own, other, share, total, partial, pieces, returned,
    q_gain, k_gain, swap, got,
    token_in, weight_in, weight_out, weight_got, swap_out, swap_got,
    share_out, share_got, relay_out, relay_got, partial_out, partial_got,
    piece_out, piece_got, context_out, context_got,
):
    scope = jax.named_scope
    dp, mp = lax.axis_index("dp"), lax.axis_index("mp")
    side, core = dp // 2, dp % 2
    quarter, group = mp // GROUPS, mp % GROUPS
    rows, features = token_hbm.shape
    depth, width = weight_hbm.shape[1:]
    half = features // 2
    images = rows // PATCHES
    part = HEAD_DIM // SPLITS
    quad_rows = PATCHES // 4
    piece_rows = quad_rows // PIECES
    small = BLOCK // SPLITS
    folded = depth // 2
    piece_lane = UNITS * BLOCK
    context_lane = 2 * piece_lane

    sibling = (side * 2 + 1 - core, mp)
    across = ((1 - side) * 2 + core, mp)
    near_group = (dp, quarter * GROUPS + 1 - group)
    near_quarter = (dp, (quarter + 1 - 2 * (quarter % 2)) * GROUPS + group)
    quad_place = (quarter % 2) * 2 + group
    near_place = (1 - quarter % 2) * 2 + group

    def quarter_at(offset):
        return (dp, (quarter + offset) % SPLITS * GROUPS + group)

    def remote(source, target, send, receive, device):
        return pltpu.make_async_remote_copy(
            src_ref=source, dst_ref=target, send_sem=send, recv_sem=receive,
            device_id=device, device_id_type=MESH,
        )

    def lines_of(image):
        return slice(image * PATCHES, (image + 1) * PATCHES)

    def token_load(image):
        lines = lines_of(image)
        return pltpu.make_async_copy(token_hbm.at[lines], work.at[lines], token_in.at[image])

    mine = span(core * depth, depth)

    def block_lanes(block):
        return slice(block * BLOCK, (block + 1) * BLOCK)

    def weight_load(block):
        columns = block_lanes(block)
        return pltpu.make_async_copy(
            weight_hbm.at[:, :, columns], weight.at[:, mine, columns], weight_in.at[block]
        )

    def weight_send(block):
        columns = block_lanes(block)
        return remote(
            weight_hbm.at[:, :, columns], weight.at[:, mine, columns],
            weight_out, weight_got.at[block], sibling,
        )

    inner = (quarter == 1) | (quarter == 2)
    partner = 3 - quarter

    def units_of(block):
        return slice(block * 3, block * 3 + 3)

    def swap_send(block):
        view = units_of(block)
        return remote(
            swap.at[view], got.at[0, view], swap_out, swap_got.at[block],
            (dp, partner * GROUPS + group),
        )

    def swap_pass(block):
        view = units_of(block)
        return remote(
            got.at[0, view], got.at[1, view],
            swap_out, swap_got.at[3 + block], sibling,
        )

    def swap_lanes(block, here):
        first = block * BLOCK + (2 * small if here == 1 else 0)
        return slice(first, first + 2 * small)

    def swap_fold():
        for here, side in ((1, 0), (2, 1)):
            @pl.when(quarter == here)
            def _(here=here, side=side):
                for unit in range(UNITS):
                    block, kind = divmod(unit, 3)
                    lanes = swap_lanes(block, here)
                    swap[unit] = jnp.concatenate(
                        [
                            weight[kind, span(core * depth + row * folded, folded), lanes][
                                :, side * small : (side + 1) * small
                            ]
                            for row in range(2)
                        ],
                        axis=1,
                    )

    def swap_unfold(block, slot):
        owner = core if slot == 0 else 1 - core
        for here, side in ((1, 0), (2, 1)):
            @pl.when(quarter == here)
            def _(here=here, side=side):
                for kind in range(3):
                    lanes = swap_lanes(block, here)
                    for row in range(2):
                        lines = span(owner * depth + row * folded, folded)
                        fresh = got[slot, block * 3 + kind][:, row * small : (row + 1) * small]
                        held = weight[kind, lines, lanes][
                            :, (1 - side) * small : (2 - side) * small
                        ]
                        both = (fresh, held) if side == 0 else (held, fresh)
                        weight[kind, lines, lanes] = jnp.concatenate(both, axis=1)

    def swap_arrive(block):
        with scope("w_swap"):
            weight_send(block).wait_recv()

            @pl.when(inner)
            def _():
                swap_send(block).wait_recv()
                swap_pass(block).start()

    def swap_finish(block):
        with scope("swap_finish"):
            @pl.when(inner)
            def _():
                swap_unfold(block, 0)
                swap_pass(block).wait_recv()
                swap_unfold(block, 1)

    def unless_swapped(offset, action):
        if offset == 2:
            action()
        else:
            pl.when(quarter != (1 if offset == 1 else 2))(action)

    def quad_view(image, place, piece=None):
        line = image * PATCHES + place * quad_rows
        if piece is None:
            return other.at[span(line, quad_rows)]
        return other.at[span(line + piece * piece_rows, piece_rows)]

    def share_slot(image, piece):
        return piece if piece is not None else PIECES + image - 1

    def share_send(image, piece=None):
        if piece is None:
            source = share.at[image * quad_rows : (image + 1) * quad_rows]
        else:
            source = share.at[span(image * quad_rows + piece * piece_rows, piece_rows)]
        slot = share_slot(image, piece)
        return remote(
            source, quad_view(image, quad_place, piece),
            share_out, share_got.at[slot], across,
        )

    def relay(image, way, piece=None):
        places = (quad_place, quad_place, near_place, quad_place + 1 - 2 * group)
        view = quad_view(image, places[way], piece)
        slot = share_slot(image, piece) * 4 + way
        device = near_group if way in (1, 2) else near_quarter
        return remote(view, view, relay_out, relay_got.at[slot], device)

    def parts_of(image, chunk):
        first = CHUNKS.index(chunk) * 3
        if (image, chunk) == (0, "a"):
            return [(unit, 1) for unit in range(first, first + 3)]
        return [(first, 3)]

    def chunk_slot(image, chunk, step):
        if image == 0:
            return step if chunk == "a" else 2 + CHUNKS.index(chunk)
        return 2 + image * 3 + CHUNKS.index(chunk)

    def partial_send(image, chunk, step):
        first, count = parts_of(image, chunk)[step]
        columns = slice(first * BLOCK, (first + count) * BLOCK)
        slot = chunk_slot(image, chunk, step)
        return remote(
            work.at[lines_of(image), columns], partial.at[image, :, columns],
            partial_out, partial_got.at[slot], across,
        )

    def piece_view(image, target, first, count):
        lane = piece_lane + first * BLOCK
        return work.at[
            span(image * PATCHES + target * small, small), slice(lane, lane + count * BLOCK)
        ]

    def piece_send(image, chunk, step, offset):
        first, count = parts_of(image, chunk)[step]
        slot = chunk_slot(image, chunk, step)
        return remote(
            piece_view(image, (quarter + offset) % SPLITS, first, count),
            pieces.at[image, quarter, :, first * BLOCK : (first + count) * BLOCK],
            piece_out, piece_got.at[slot], quarter_at(offset),
        )

    def context_view(image, chunk, target):
        lane = context_lane + CHUNKS.index(chunk) * BLOCK
        return work.at[span(image * PATCHES + target * small, small), slice(lane, lane + BLOCK)]

    def context_send(image, chunk, offset):
        slot = image * 3 + CHUNKS.index(chunk)
        return remote(
            context_view(image, chunk, (quarter + offset) % SPLITS),
            returned.at[image, CHUNKS.index(chunk), quarter],
            context_out, context_got.at[slot], quarter_at(offset),
        )

    own_half = span(side * half, half)
    other_half = span((1 - side) * half, half)

    def normalize(line, count, share_line=None):
        lines = span(line, count)
        values = work[lines, :].astype(jnp.float32)
        centre = jnp.mean(values, axis=-1, keepdims=True)
        centred = values - centre
        spread = jnp.mean(centred * centred, axis=-1, keepdims=True)
        scale = lax.rsqrt(spread + norm_eps)

        def scaled(columns):
            return (
                (work[lines, columns].astype(jnp.float32) - centre) * scale * gain_ref[:, columns]
            ).astype(jnp.bfloat16)

        if share_line is not None:
            share[span(share_line, count), :] = scaled(other_half)
        own[lines, :] = scaled(own_half)

    def own_part(block, step):
        with scope("own_part"):
            total[:, span((block * 3 + step) * BLOCK, BLOCK)] = jnp.dot(
                own[...], weight[step, :, block_lanes(block)], preferred_element_type=jnp.float32
            )

    def own_chunk(chunk):
        def looped(step, carry):
            own_part(CHUNKS.index(chunk), step)
            return carry

        lax.fori_loop(0, 3, looped, 0)

    def send_partial(image, chunk):
        block = CHUNKS.index(chunk)
        split = len(parts_of(image, chunk)) > 1

        def other_part(step):
            work[lines_of(image), span((block * 3 + step) * BLOCK, BLOCK)] = jnp.dot(
                other[lines_of(image), :], weight[step, :, block_lanes(block)],
                preferred_element_type=jnp.float32,
            ).astype(jnp.bfloat16)

        def looped(step, carry):
            other_part(step)
            return carry

        with scope(f"other_part_{image}{chunk}"):
            if split:
                for step in range(3):
                    other_part(step)
                    partial_send(image, chunk, step).start()
            else:
                lax.fori_loop(0, 3, looped, 0)
                partial_send(image, chunk, 0).start()

    def sum_step(image, chunk, step):
        first, count = parts_of(image, chunk)[step]
        with scope(f"w_partial_{image}{chunk}"):
            partial_send(image, chunk, step).wait_recv()
        for unit in range(first, first + count):
            columns = slice(unit * BLOCK, (unit + 1) * BLOCK)
            whole = total[lines_of(image), columns] + partial[image, :, columns].astype(
                jnp.float32
            )
            work[
                lines_of(image), piece_lane + unit * BLOCK : piece_lane + (unit + 1) * BLOCK
            ] = whole.T.astype(jnp.bfloat16)
        for offset in (2, 1, 3):
            unless_swapped(
                offset, lambda offset=offset: piece_send(image, chunk, step, offset).start()
            )

    def sum_up(image, chunk):
        for step in range(len(parts_of(image, chunk))):
            sum_step(image, chunk, step)
        first = CHUNKS.index(chunk) * 3
        lanes = slice(first * BLOCK, (first + 3) * BLOCK)
        pieces[image, quarter, :, lanes] = piece_view(image, quarter, first, 3)[...]

        @pl.when(inner)
        def _():
            pieces[image, partner, :, lanes] = piece_view(image, partner, first, 3)[...]

    def attend(image, chunk):
        with scope(f"w_piece_{image}{chunk}"):
            for step, (first, count) in enumerate(parts_of(image, chunk)):
                slot = chunk_slot(image, chunk, step)
                lanes = slice(first * BLOCK, (first + count) * BLOCK)
                for number, condition in ((2, inner), (3, jnp.logical_not(inner))):
                    @pl.when(condition)
                    def _(number=number, slot=slot, lanes=lanes):
                        view = pieces.at[image, :number, :, lanes]
                        remote(
                            view, view, piece_out, piece_got.at[slot], quarter_at(1)
                        ).wait_recv()

        def gathered(head, kind):
            lane = (CHUNKS.index(chunk) * 3 + kind) * BLOCK
            lines = slice(head * part, (head + 1) * part)
            found = [pieces[image, source, lines, lane : lane + BLOCK] for source in range(SPLITS)]
            return jnp.concatenate(found, axis=0)

        with scope(f"attend_{image}{chunk}"):
            for head in range(small // part):
                query = (
                    column_norm(gathered(head, 0).astype(jnp.float32), q_gain[...])
                    * HEAD_DIM ** (-0.5)
                ).astype(jnp.bfloat16)
                key = column_norm(gathered(head, 1).astype(jnp.float32), k_gain[...]).astype(
                    jnp.bfloat16
                )
                scores = lax.dot_general(
                    key, query, (((0,), (0,)), ((), ())), preferred_element_type=jnp.float32
                )
                raised = jnp.exp(scores)
                weights = (raised / jnp.sum(raised, axis=0, keepdims=True)).astype(jnp.bfloat16)
                attended = jnp.dot(
                    gathered(head, 2), weights, preferred_element_type=jnp.float32
                ).astype(jnp.bfloat16)
                lane = context_lane + CHUNKS.index(chunk) * BLOCK
                for target in range(SPLITS):
                    line = image * PATCHES + target * small + head * part
                    work[line : line + part, lane : lane + BLOCK] = attended[
                        target * part : (target + 1) * part
                    ]
        for offset in (2, 1, 3):
            context_send(image, chunk, offset).start()
        returned[image, CHUNKS.index(chunk), quarter] = context_view(image, chunk, quarter)[...]

    def store(image, chunk):
        block = CHUNKS.index(chunk)
        with scope(f"w_context_{image}{chunk}"):
            view = returned.at[image, block, : SPLITS - 1]
            remote(
                view, view, context_out, context_got.at[image * 3 + block], quarter_at(1)
            ).wait_recv()
        out_ref[lines_of(image), block * BLOCK : (block + 1) * BLOCK] = (
            returned[image, block].reshape(BLOCK, PATCHES).T
        )

    def token_ready(image):
        with scope(f"w_token_{image}"):
            if image == 0:
                for piece in range(PIECES):
                    if piece < PIECES // 2:
                        relay(image, 1, piece).wait_recv()
                        relay(image, 2, piece).wait_recv()
                    else:
                        relay(image, 0, piece).wait_recv()
                        relay(image, 3, piece).wait_recv()
            else:
                relay(image, 1).wait_recv()
                relay(image, 2).wait_recv()

    def pass_quarter(image, piece=None):
        with scope(f"w_share_{image}"):
            share_send(image, piece).wait_recv()
        relay(image, 0, piece).start()

    def pass_group(image, piece=None):
        relay(image, 1, piece).start()

    def pass_near(image, piece=None):
        with scope(f"w_near_{image}"):
            relay(image, 0, piece).wait_recv()
        relay(image, 2, piece).start()

    def pass_side(image, piece):
        with scope(f"w_side_{image}"):
            relay(image, 1, piece).wait_recv()
        relay(image, 3, piece).start()

    def drain(view, semaphore):
        remote(view, view, semaphore, weight_got.at[0], sibling).wait_send()

    barrier = pltpu.get_barrier_semaphore()
    partners = [sibling, across, near_group] + [quarter_at(o) for o in range(1, SPLITS)]
    for device in partners:
        pl.semaphore_signal(barrier, inc=1, device_id=device, device_id_type=MESH)
    token_load(0).start()
    for block in range(3):
        weight_load(block).start()
    for image in range(1, images):
        token_load(image).start()
    q_gain[...] = jnp.broadcast_to(q_gain_ref[...], (PATCHES, HEAD_DIM)).T
    k_gain[...] = jnp.broadcast_to(k_gain_ref[...], (PATCHES, HEAD_DIM)).T

    def share_norm(image, carry):
        normalize(image * PATCHES + quad_place * quad_rows, quad_rows, image * quad_rows)
        return carry

    token_load(0).wait()
    with scope("norm_share_0"):
        share_norm(0, 0)
    with scope("barrier"):
        pl.semaphore_wait(barrier, len(partners))
    for piece in range(PIECES):
        share_send(0, piece).start()
    weight_send(0).start()
    for block in range(3):
        weight_load(block).wait()
    with scope("fold"):
        swap_fold()

    @pl.when(inner)
    def _():
        for block in range(3):
            swap_send(block).start()

    token_load(1).wait()
    token_load(2).wait()
    with scope("norm_share"):
        lax.fori_loop(1, images, share_norm, 0)
    for image in range(1, images):
        share_send(image).start()
    weight_send(1).start()
    weight_send(2).start()

    def rest_norm(image, step, carry):
        normalize(image * PATCHES + (quad_place + step + 1) % 4 * quad_rows, quad_rows)
        return carry

    def rest_image(image, carry):
        with scope("norm_rest"):
            lax.fori_loop(0, 3, functools.partial(rest_norm, image), 0)

        @pl.when(image > 0)
        def _():
            pass_quarter(0, image - 1)
            pass_group(0, image - 1)

        return carry

    lax.fori_loop(0, images, rest_image, 0)
    pass_quarter(0, 2)
    pass_group(0, 2)
    pass_quarter(0, 3)
    pass_group(0, 3)
    pass_near(0, 0)
    pass_near(0, 1)
    swap_arrive(0)
    pass_side(0, 2)
    pass_side(0, 3)
    swap_finish(0)
    pass_quarter(1)
    pass_group(1)
    own_chunk("a")
    token_ready(0)
    send_partial(0, "a")
    swap_arrive(1)
    swap_finish(1)
    send_partial(0, "b")
    pass_quarter(2)
    sum_up(0, "a")
    own_chunk("b")
    pass_near(1)
    pass_group(2)
    swap_arrive(2)
    swap_finish(2)
    send_partial(0, "d")
    sum_up(0, "b")
    own_chunk("d")
    token_ready(1)
    send_partial(1, "a")
    send_partial(1, "b")
    send_partial(1, "d")
    attend(0, "a")
    sum_up(0, "d")
    pass_near(2)
    sum_up(1, "a")
    token_ready(2)
    send_partial(2, "a")
    send_partial(2, "b")
    send_partial(2, "d")
    attend(0, "b")
    sum_up(1, "b")
    attend(0, "d")
    sum_up(1, "d")
    attend(1, "a")
    sum_up(2, "a")
    attend(1, "b")
    sum_up(2, "b")
    attend(1, "d")
    sum_up(2, "d")
    attend(2, "a")
    for chunk in CHUNKS:
        store(0, chunk)
    store(1, "a")
    attend(2, "b")
    store(1, "b")
    attend(2, "d")
    store(1, "d")
    for chunk in CHUNKS:
        store(2, chunk)

    drain(weight.at[:, mine, :], weight_out)
    drain(share, share_out)
    drain(other.at[: images * 3 * quad_rows], relay_out)
    drain(work.at[:, :piece_lane], partial_out)
    drain(work.at[: images * small, :piece_lane], context_out)

    @pl.when(inner)
    def _():
        drain(got, swap_out)
        drain(work.at[: images * 2 * small, :piece_lane], piece_out)

    @pl.when(jnp.logical_not(inner))
    def _():
        drain(work.at[: images * 3 * small, :piece_lane], piece_out)


def fused(tokens, gain, weights, q_gain, k_gain):
    rows, features = tokens.shape
    kinds, depth, width = weights.shape
    images = rows // PATCHES
    small = BLOCK // SPLITS
    whole = pl.BlockSpec(memory_space=pltpu.VMEM)
    outside = pl.BlockSpec(memory_space=pl.ANY)
    dma = pltpu.SemaphoreType.DMA

    def vmem(*shape, dtype=jnp.bfloat16):
        return pltpu.VMEM(shape, dtype)

    share_count = PIECES + images - 1
    chunk_count = images * 3 + 2
    return pl.pallas_call(
        fused_kernel,
        out_shape=jax.ShapeDtypeStruct((rows, width), jnp.bfloat16),
        in_specs=[outside, whole, outside, whole, whole],
        out_specs=whole,
        scratch_shapes=[
            vmem(rows, features),
            vmem(kinds, 2 * depth, width),
            vmem(rows, features // 2),
            vmem(rows, features // 2),
            vmem(images * PATCHES // 4, features // 2),
            vmem(rows, kinds * width, dtype=jnp.float32),
            vmem(images, PATCHES, kinds * width),
            vmem(images, SPLITS, small, UNITS * PATCHES),
            vmem(images, 3, SPLITS, small, PATCHES),
            vmem(HEAD_DIM, PATCHES, dtype=jnp.float32),
            vmem(HEAD_DIM, PATCHES, dtype=jnp.float32),
            vmem(UNITS, depth // 2, 2 * small),
            vmem(2, UNITS, depth // 2, 2 * small),
            dma((images,)), dma((3,)), dma, dma((3,)),
            dma, dma((6,)),
            dma, dma((share_count,)),
            dma, dma((4 * share_count,)),
            dma, dma((chunk_count,)),
            dma, dma((chunk_count,)),
            dma, dma((images * 3,)),
        ],
        compiler_params=pltpu.CompilerParams(
            collective_id=0, has_side_effects=True, vmem_limit_bytes=VMEM_LIMIT
        ),
        name="fused",
    )(tokens, gain.reshape(1, features), weights, q_gain.reshape(1, HEAD_DIM),
      k_gain.reshape(1, HEAD_DIM))


def body(tokens, ln_gain, w_qkv, q_gain, k_gain):
    fits = lax.axis_size("dp") == 4 and lax.axis_size("mp") == GROUPS * SPLITS
    fits = fits and tokens.shape == (3 * PATCHES, 4 * w_qkv.shape[0])
    fits = fits and w_qkv.shape[1:] == (3, 3 * BLOCK) and w_qkv.shape[0] % BLOCK == 0
    if not fits:
        return plain_body(tokens, ln_gain, w_qkv, q_gain, k_gain)
    return fused(tokens, ln_gain, jnp.transpose(w_qkv, (1, 0, 2)), q_gain, k_gain)


def solution(mesh):
    return jax.shard_map(
        body,
        mesh=mesh,
        in_specs=(P("dp", None), P(), P("dp", None, "mp"), P(), P()),
        out_specs=P("dp", "mp"),
        check_vma=False,
    )
```

time: 170 us -> 140 us (0.82)
  Pallas kernels: 165 us -> 137 us
  local copies, waits for them, and re-layouts: 5.13 us -> 2.36 us
    pallas_call x1, Pallas kernels: 165 us -> 137 us  [fused(): pl.pallas_call(fused_kernel, out_shape=jax.ShapeDtypeStruct((rows, width)...]
    reshape x2 -> x0, local copies, waits for them, and re-layouts: 2.77 us -> none  [the longest x1 1.39 us: fused(): q_gain.reshape(HEAD_DIM, 1)]
where the time goes in v1:
time: 140 us
  Pallas kernels  137 us (98%)
  local copies, waits for them, and re-layouts  2.36 us (2%)
    pallas_call x1, Pallas kernels, fused(): pl.pallas_call(fused_kernel, out_shape=jax.ShapeDtypeStruct((rows, width)...  137 us

profile of v1, /device:TPU:0, one launch (start us, length us, event | category | flops | bytes accessed | tf_op | source)
XLA Modules:
  0.0 139.6 jit_solution(5363023337849171665)
XLA Ops:
  0.0 137.2 %fused.1 = bf16[768,768]{1,0:T(8,128)(2,1)} custom-call(bf16[768,6144]{1,0:T(8,128)(2,1)} %token_hbm.1, f32[1,6144]{1,0:T(1,128)} %bitcast.5, bf16[3,1536,768]{2,1,0:T(8,128)(2,1)} %bitcast.4, f32[1,128]{1,0:T(1,128)} %bitcast.6, f32[1,128]{1,0:T(1,128)} %bitcast.7), custom_call_target="tpu_custom_call" | custom-call | tf_op jit(solution)/shard_map/fused/pallas_call | solution.py:669
  137.3 2.4 %copy.7 = bf16[768,768]{1,0:T(8,128)(2,1)} copy(bf16[768,768]{1,0:T(8,128)(2,1)} %fused.1) | data formatting | bytes 2359296

commit v2 on v1

--- a/solution.py
+++ b/solution.py
@@ -108,6 +108,7 @@
 GROUPS = 2
 UNITS = 9
 CHUNKS = "abd"
+SWAPPED = "abd"
 
 
 def column_norm(values, gain):
@@ -168,6 +169,20 @@
         lines = lines_of(image)
         return pltpu.make_async_copy(token_hbm.at[lines], work.at[lines], token_in.at[image])
 
+    def quarter_load(turn, semaphore):
+        lines = span((quad_place + turn) % 4 * quad_rows, quad_rows)
+        return pltpu.make_async_copy(token_hbm.at[lines], work.at[lines], semaphore)
+
+    def first_load():
+        return quarter_load(0, token_in.at[0])
+
+    def rest_load(turn):
+        return quarter_load(turn, token_in.at[3])
+
+    def rest_wait():
+        lines = slice(0, 3 * quad_rows)
+        pltpu.make_async_copy(token_hbm.at[lines], work.at[lines], token_in.at[3]).wait()
+
     mine = span(core * depth, depth)
 
     def block_lanes(block):
@@ -214,7 +229,7 @@
         for here, side in ((1, 0), (2, 1)):
             @pl.when(quarter == here)
             def _(here=here, side=side):
-                for unit in range(UNITS):
+                for unit in range(3 * len(SWAPPED)):
                     block, kind = divmod(unit, 3)
                     lanes = swap_lanes(block, here)
                     swap[unit] = jnp.concatenate(
@@ -244,6 +259,9 @@
                         weight[kind, lines, lanes] = jnp.concatenate(both, axis=1)
 
     def swap_arrive(block):
+        if block >= len(SWAPPED):
+            weight_send(block).wait_recv()
+            return
         with scope("w_swap"):
             weight_send(block).wait_recv()
 
@@ -253,6 +271,8 @@
                 swap_pass(block).start()
 
     def swap_finish(block):
+        if block >= len(SWAPPED):
+            return
         with scope("swap_finish"):
             @pl.when(inner)
             def _():
@@ -260,8 +280,8 @@
                 swap_pass(block).wait_recv()
                 swap_unfold(block, 1)
 
-    def unless_swapped(offset, action):
-        if offset == 2:
+    def unless_swapped(chunk, offset, action):
+        if offset == 2 or chunk not in SWAPPED:
             action()
         else:
             pl.when(quarter != (1 if offset == 1 else 2))(action)
@@ -410,32 +430,39 @@
             ] = whole.T.astype(jnp.bfloat16)
         for offset in (2, 1, 3):
             unless_swapped(
-                offset, lambda offset=offset: piece_send(image, chunk, step, offset).start()
+                chunk, offset, lambda offset=offset: piece_send(image, chunk, step, offset).start()
             )
 
     def sum_up(image, chunk):
         for step in range(len(parts_of(image, chunk))):
             sum_step(image, chunk, step)
+        sum_keep(image, chunk)
+
+    def sum_keep(image, chunk):
         first = CHUNKS.index(chunk) * 3
         lanes = slice(first * BLOCK, (first + 3) * BLOCK)
         pieces[image, quarter, :, lanes] = piece_view(image, quarter, first, 3)[...]
 
-        @pl.when(inner)
-        def _():
-            pieces[image, partner, :, lanes] = piece_view(image, partner, first, 3)[...]
+        if chunk in SWAPPED:
+            @pl.when(inner)
+            def _():
+                pieces[image, partner, :, lanes] = piece_view(image, partner, first, 3)[...]
 
     def attend(image, chunk):
         with scope(f"w_piece_{image}{chunk}"):
             for step, (first, count) in enumerate(parts_of(image, chunk)):
                 slot = chunk_slot(image, chunk, step)
                 lanes = slice(first * BLOCK, (first + count) * BLOCK)
-                for number, condition in ((2, inner), (3, jnp.logical_not(inner))):
-                    @pl.when(condition)
-                    def _(number=number, slot=slot, lanes=lanes):
-                        view = pieces.at[image, :number, :, lanes]
-                        remote(
-                            view, view, piece_out, piece_got.at[slot], quarter_at(1)
-                        ).wait_recv()
+
+                def wait_for(number, slot=slot, lanes=lanes):
+                    view = pieces.at[image, :number, :, lanes]
+                    remote(view, view, piece_out, piece_got.at[slot], quarter_at(1)).wait_recv()
+
+                if chunk in SWAPPED:
+                    pl.when(inner)(functools.partial(wait_for, SPLITS - 2))
+                    pl.when(jnp.logical_not(inner))(functools.partial(wait_for, SPLITS - 1))
+                else:
+                    wait_for(SPLITS - 1)
 
         def gathered(head, kind):
             lane = (CHUNKS.index(chunk) * 3 + kind) * BLOCK
@@ -520,7 +547,10 @@
     partners = [sibling, across, near_group] + [quarter_at(o) for o in range(1, SPLITS)]
     for device in partners:
         pl.semaphore_signal(barrier, inc=1, device_id=device, device_id_type=MESH)
-    token_load(0).start()
+    first_load().start()
+    rest_load(1).start()
+    rest_load(2).start()
+    rest_load(3).start()
     for block in range(3):
         weight_load(block).start()
     for image in range(1, images):
@@ -532,7 +562,7 @@
         normalize(image * PATCHES + quad_place * quad_rows, quad_rows, image * quad_rows)
         return carry
 
-    token_load(0).wait()
+    first_load().wait()
     with scope("norm_share_0"):
         share_norm(0, 0)
     with scope("barrier"):
@@ -547,9 +577,10 @@
 
     @pl.when(inner)
     def _():
-        for block in range(3):
+        for block in range(len(SWAPPED)):
             swap_send(block).start()
 
+    rest_wait()
     token_load(1).wait()
     token_load(2).wait()
     with scope("norm_share"):
@@ -587,35 +618,38 @@
     swap_finish(0)
     pass_quarter(1)
     pass_group(1)
-    own_chunk("a")
     token_ready(0)
     send_partial(0, "a")
+    own_chunk("a")
+    sum_step(0, "a", 0)
     swap_arrive(1)
     swap_finish(1)
     send_partial(0, "b")
+    pass_near(1)
+    sum_step(0, "a", 1)
+    sum_step(0, "a", 2)
+    sum_keep(0, "a")
     pass_quarter(2)
-    sum_up(0, "a")
+    pass_group(2)
     own_chunk("b")
-    pass_near(1)
-    pass_group(2)
     swap_arrive(2)
     swap_finish(2)
     send_partial(0, "d")
     sum_up(0, "b")
-    own_chunk("d")
     token_ready(1)
     send_partial(1, "a")
     send_partial(1, "b")
     send_partial(1, "d")
+    own_chunk("d")
     attend(0, "a")
+    pass_near(2)
     sum_up(0, "d")
-    pass_near(2)
     sum_up(1, "a")
+    attend(0, "b")
     token_ready(2)
     send_partial(2, "a")
     send_partial(2, "b")
     send_partial(2, "d")
-    attend(0, "b")
     sum_up(1, "b")
     attend(0, "d")
     sum_up(1, "d")
@@ -645,7 +679,8 @@
     @pl.when(inner)
     def _():
         drain(got, swap_out)
-        drain(work.at[: images * 2 * small, :piece_lane], piece_out)
+        fewer = len(SWAPPED) * small
+        drain(work.at[: images * 3 * small - images * fewer // 3, :piece_lane], piece_out)
 
     @pl.when(jnp.logical_not(inner))
     def _():
@@ -683,9 +718,9 @@
             vmem(images, 3, SPLITS, small, PATCHES),
             vmem(HEAD_DIM, PATCHES, dtype=jnp.float32),
             vmem(HEAD_DIM, PATCHES, dtype=jnp.float32),
-            vmem(UNITS, depth // 2, 2 * small),
-            vmem(2, UNITS, depth // 2, 2 * small),
-            dma((images,)), dma((3,)), dma, dma((3,)),
+            vmem(3 * len(SWAPPED), depth // 2, 2 * small),
+            vmem(2, 3 * len(SWAPPED), depth // 2, 2 * small),
+            dma((images + 1,)), dma((3,)), dma, dma((3,)),
             dma, dma((6,)),
             dma, dma((share_count,)),
             dma, dma((4 * share_count,)),

time: 140 us -> 137 us (0.979)
  Pallas kernels: 137 us -> 134 us
    pallas_call x1, Pallas kernels: 137 us -> 134 us  [fused(): pl.pallas_call(fused_kernel, out_shape=jax.ShapeDtypeStruct((rows, width)...]
where the time goes in v2:
time: 137 us
  Pallas kernels  134 us (98%)
  local copies, waits for them, and re-layouts  2.36 us (2%)
    pallas_call x1, Pallas kernels, fused(): pl.pallas_call(fused_kernel, out_shape=jax.ShapeDtypeStruct((rows, width)...  134 us

profile of v2, /device:TPU:0, one launch (start us, length us, event | category | flops | bytes accessed | tf_op | source)
XLA Modules:
  0.0 136.7 jit_solution(10143795112070868127)
XLA Ops:
  0.0 134.3 %fused.1 = bf16[768,768]{1,0:T(8,128)(2,1)} custom-call(bf16[768,6144]{1,0:T(8,128)(2,1)} %token_hbm.1, f32[1,6144]{1,0:T(1,128)} %bitcast.5, bf16[3,1536,768]{2,1,0:T(8,128)(2,1)} %bitcast.4, f32[1,128]{1,0:T(1,128)} %bitcast.6, f32[1,128]{1,0:T(1,128)} %bitcast.7), custom_call_target="tpu_custom_call" | custom-call | tf_op jit(solution)/shard_map/fused/pallas_call | solution.py:704
  134.3 2.4 %copy.7 = bf16[768,768]{1,0:T(8,128)(2,1)} copy(bf16[768,768]{1,0:T(8,128)(2,1)} %fused.1) | data formatting | bytes 2359296

commit v3 on v2

--- a/solution.py
+++ b/solution.py
@@ -315,14 +315,17 @@
 
     def parts_of(image, chunk):
         first = CHUNKS.index(chunk) * 3
-        if (image, chunk) == (0, "a"):
+        if (image, chunk) in ((0, "a"), (images - 1, CHUNKS[-1])):
             return [(unit, 1) for unit in range(first, first + 3)]
         return [(first, 3)]
 
     def chunk_slot(image, chunk, step):
-        if image == 0:
-            return step if chunk == "a" else 2 + CHUNKS.index(chunk)
-        return 2 + image * 3 + CHUNKS.index(chunk)
+        slot = step
+        for earlier in range(images):
+            for other_chunk in CHUNKS:
+                if (earlier, other_chunk) == (image, chunk):
+                    return slot
+                slot += len(parts_of(earlier, other_chunk))
 
     def partial_send(image, chunk, step):
         first, count = parts_of(image, chunk)[step]
@@ -700,7 +703,7 @@
         return pltpu.VMEM(shape, dtype)
 
     share_count = PIECES + images - 1
-    chunk_count = images * 3 + 2
+    chunk_count = images * 3 + 4
     return pl.pallas_call(
         fused_kernel,
         out_shape=jax.ShapeDtypeStruct((rows, width), jnp.bfloat16),

time: 137 us -> 137 us (level)
  no operation moved by 1% of the time
where the time goes in v3:
time: 137 us
  Pallas kernels  134 us (98%)
  local copies, waits for them, and re-layouts  2.36 us (2%)
    pallas_call x1, Pallas kernels, fused(): pl.pallas_call(fused_kernel, out_shape=jax.ShapeDtypeStruct((rows, width)...  134 us

profile of v3, /device:TPU:0, one launch (start us, length us, event | category | flops | bytes accessed | tf_op | source)
XLA Modules:
  0.0 136.7 jit_solution(14777204773523000267)
XLA Ops:
  0.0 134.3 %fused.1 = bf16[768,768]{1,0:T(8,128)(2,1)} custom-call(bf16[768,6144]{1,0:T(8,128)(2,1)} %token_hbm.1, f32[1,6144]{1,0:T(1,128)} %bitcast.5, bf16[3,1536,768]{2,1,0:T(8,128)(2,1)} %bitcast.4, f32[1,128]{1,0:T(1,128)} %bitcast.6, f32[1,128]{1,0:T(1,128)} %bitcast.7), custom_call_target="tpu_custom_call" | custom-call | tf_op jit(solution)/shard_map/fused/pallas_call | solution.py:707
  134.3 2.4 %copy.7 = bf16[768,768]{1,0:T(8,128)(2,1)} copy(bf16[768,768]{1,0:T(8,128)(2,1)} %fused.1) | data formatting | bytes 2359296
